TPU v7x, 32 devices: a whole 2x2x4 slice. The times are simulated.
32 devices in a mesh: gx: 2 (over y), gy: 4 (over x, core), gz: 4 (over z).
Axes of the slice: x: 2, y: 2, z: 4, core: 2. Of those that a mesh axis runs over, the one named last changes fastest.
Arguments:
- volume: float32 [16, 64, 512], P(('gx', 'gy'), None, 'gz'), may hold values from 0 to 1
- levels: int32 [4], replicated, may hold values from 0 to 255
Outputs:
- labelling: float32 [4, 16, 64, 512], P(None, 'gx', 'gy', 'gz')
- centers: float32 [4], replicated
All inputs are finite; a program needn't handle non-finite values.
Results may differ from a plain program's by a relative error of at most 0.0001.
Values sent between devices are 32-bit elements; how exact they have to be, the bound alone decides.
No kernel may reach another device: no remote copies, remote signals or barrier semaphores. Data moves between devices by JAX's collectives and lax.ppermute only.
A program may use at most 64 MiB of HBM per device.

v0:
```python
import functools

import jax
import jax.numpy as jnp
from jax import lax
from jax.experimental import pallas as pl
from jax.experimental.pallas import tpu as pltpu
from jax.sharding import PartitionSpec as P


tau_step = 0.25
prior_weight = 1.0


AXES = ("gy", "gx", "gz")
SLABS = ("gx", "gy")
ROWS = 5


def project_simplex(values, total):
    a, b, c, d = values
    a, b = jnp.maximum(a, b), jnp.minimum(a, b)
    c, d = jnp.maximum(c, d), jnp.minimum(c, d)
    a, c = jnp.maximum(a, c), jnp.minimum(a, c)
    b, d = jnp.maximum(b, d), jnp.minimum(b, d)
    b, c = jnp.maximum(b, c), jnp.minimum(b, c)
    one = a - total
    two = one + b
    three = two + c
    four = three + d
    threshold = jnp.maximum(
        jnp.maximum(one, two * 0.5), jnp.maximum(three * (1.0 / 3.0), four * 0.25)
    )
    return [jnp.maximum(value - threshold, 0.0) for value in values]


def affine(centers, unit):
    return [
        (center * (2.0 * unit * tau_step), center * center * (unit * tau_step))
        for center in centers
    ]


def attraction(volume, terms):
    return [volume * slope - offset for slope, offset in terms]


def shrink_of(x, y, z):
    return lax.rsqrt(jnp.maximum(x * x + y * y + z * z, 1.0))


class Planes:
    def __init__(self, shape, height, x_first, x_total):
        self.height = height
        self.rows, self.lanes = shape
        lane = lax.broadcasted_iota(jnp.int32, shape, 1)
        self.low = lane < height
        y = jnp.where(self.low, lane, lane - height)
        x = x_first + jnp.where(self.low, 0, 1)
        self.open_x = (x != x_total - 1).astype(jnp.float32)
        self.open_y = (y != height - 1).astype(jnp.float32)
        self.inside = (x >= 0).astype(jnp.float32)

    def dual(self, value, next_z, old=None):
        swapped = pltpu.roll(value, self.height, 1)
        following = jnp.where(self.low, swapped, pltpu.roll(swapped, self.rows - 1, 0))
        x = (following - value) * self.open_x
        y = (pltpu.roll(value, self.lanes - 1, 1) - value) * self.open_y
        z = next_z - value
        if old is not None:
            x, y, z = old[0] + x, old[1] + y, old[2] + z
        shrink = shrink_of(x, y, z)
        return x * shrink, y * shrink, z * shrink

    def behind_xy(self, x, y):
        swapped = pltpu.roll(x, self.height, 1)
        before_x = jnp.where(self.low, pltpu.roll(swapped, 1, 0), swapped)
        return (x - before_x) + (y - pltpu.roll(y, 1, 1))


def total_of(value):
    return jnp.sum(jnp.sum(value, axis=0, keepdims=True), axis=1, keepdims=True)


def base_kernel(levels_ref, base_ref):
    values = levels_ref[...].astype(jnp.float32) / 255.0
    for label in range(values.shape[1]):
        base_ref[label : label + 1] = jnp.broadcast_to(
            values[:, label : label + 1], (1, base_ref.shape[1])
        )


def base_of(base_ref):
    return [base_ref[label : label + 1] for label in range(base_ref.shape[0])]


def pack_sums(sums, shape):
    lane = lax.broadcasted_iota(jnp.int32, shape, 1)
    row = jnp.zeros(shape, jnp.float32)
    for index, value in enumerate(sums):
        row = jnp.where(lane == index, total_of(value), row)
    return row


def rank_of(slab):
    count = lax.axis_size("gy")
    return lax.rem(slab, count) * lax.axis_size("gx") + slab // count


def slab_index():
    return lax.axis_index("gx") * lax.axis_size("gy") + lax.axis_index("gy")


def open_lanes(depth):
    lane = lax.broadcasted_iota(jnp.int32, (1, depth), 1)
    return (lane != depth - 1).astype(jnp.float32)


def volume_layers(v_ref, pair_ref, other_ref, halo):
    thick = v_ref.shape[0]
    odd = lax.rem(slab_index(), 2) == 1

    def read(layer, rows=slice(None)):
        if layer < halo:
            layer += thick - halo
            return jnp.where(odd, pair_ref[layer, rows], other_ref[layer, rows])
        layer -= halo
        if layer < thick:
            return v_ref[layer, rows]
        layer -= thick
        return jnp.where(odd, other_ref[layer, rows], pair_ref[layer, rows])

    return read


def add_to(sums, index, term):
    sums[index] = term if sums[index] is None else sums[index] + term


CHUNK = 16
COVER = 50_000_000


def store_padded(ref, where, start, value, height):
    rows = value.shape[0]
    ref[where + (slice(start, start + rows),)] = value
    if start + rows == height:
        ref[where + (slice(height, height + 1),)] = value[rows - 1 :]


def first_halves(read, layers, height, terms, h_ref):
    for layer in layers:
        for start in range(0, height, CHUNK):
            values = read(layer, slice(start, start + CHUNK))
            for label, half in enumerate(project_simplex(attraction(values, terms), 0.5)):
                store_padded(h_ref, (label, layer), start, half, height)


def gradient(h_ref, label, layer, height, depth, open_z):
    half = h_ref[label, layer, 0:height]
    x = h_ref[label, layer + 1, 0:height] - half
    y = h_ref[label, layer, 1 : height + 1] - half
    z = (pltpu.roll(half, depth - 1, 1) - half) * open_z
    return x, y, z


def behind_yz(y, z, y_ref, where, height):
    y_ref[where + (slice(0, 8),)] = jnp.zeros((8, y.shape[1]), jnp.float32)
    y_ref[where + (slice(8, 8 + height),)] = y
    return (y - y_ref[where + (slice(7, 7 + height),)]) + (z - pltpu.roll(z, 1, 1))


def pair_kernel(v_ref, pair_ref, base_ref, h_ref, e_ref, sums_ref, planes_ref, y_ref, d_ref, b_ref):
    thick, height, depth = v_ref.shape
    lanes = thick * height
    labels = base_ref.shape[0]
    terms = affine(base_of(base_ref), 0.5)
    open_z = open_lanes(depth)
    odd = lax.rem(slab_index(), 2)
    sign = (1 - 2 * odd).astype(jnp.float32) * 0.0625
    even = (1 - odd).astype(jnp.float32) * 0.0625
    near = odd * (thick - 1)

    def read(layer, rows):
        return v_ref[layer, rows] if layer < thick else pair_ref[near, rows]

    first_halves(read, range(thick + 1), height, terms, h_ref)
    turned = jnp.transpose(v_ref[...].reshape(lanes, depth))
    planes_ref[0:2] = turned[0:2]
    planes_ref[2:4] = turned[depth - 2 : depth]
    at = jnp.where(odd == 1, 2, 1)
    following = jnp.where(odd == 1, 0, 2)
    done = 1 - odd
    for label in range(labels):
        for index, (layer, after) in enumerate(((0, 1), (at, following))):
            half = h_ref[label, layer, 0:height]
            x = h_ref[label, after, 0:height] - half
            y = h_ref[label, layer, 1 : height + 1] - half
            z = (pltpu.roll(half, depth - 1, 1) - half) * open_z
            shrink = shrink_of(x, y, z)
            d_ref[label, index] = x * shrink
            b_ref[label, index] = behind_yz(
                y * shrink, z * shrink, y_ref, (label, index), height
            )
    sums = [None] * (2 * labels)
    for start in range(0, height, CHUNK):
        rows = slice(start, start + CHUNK)
        values = v_ref[done, rows]
        entries = []
        for label, term in enumerate(attraction(values, terms)):
            across = sign * (d_ref[label, 1, rows] - d_ref[label, 0, rows])
            along = 0.0625 * b_ref[label, done, rows]
            entries.append(h_ref[label, done, rows] + term + (across + along))
        for label, value in enumerate(project_simplex(entries, 0.5)):
            add_to(sums, label, value)
            add_to(sums, labels + label, value * values)
        values = v_ref[odd, rows]
        for label, term in enumerate(attraction(values, terms)):
            part = sign * d_ref[label, 0, rows] + even * b_ref[label, 0, rows]
            e_ref[label, rows] = h_ref[label, odd, rows] + term + part
    for index, value in enumerate(sums):
        sums_ref[index] = value


def first_kernel(
    v_ref, other_ref, base_ref, h_ref, e_ref, sums_in, planes_ref, out_ref, n_ref, y_ref
):
    slabs = lax.axis_size(SLABS)
    blocks = lax.axis_size("gz")
    slab, block = slab_index(), lax.axis_index("gz")
    thick, height, depth = v_ref.shape
    lanes = thick * height
    devices = slabs * blocks
    labels = base_ref.shape[0]
    terms = affine(base_of(base_ref), 0.5)
    open_z = open_lanes(depth)
    odd = lax.rem(slab, 2)
    is_odd = odd == 1
    left = (1 - odd) * (thick - 1)

    for row in range(ROWS - 1):
        out_ref[pl.ds(row, devices, stride=ROWS), :] = jnp.broadcast_to(
            planes_ref[row : row + 1], (devices, lanes)
        )
    open_x = jnp.where(is_odd & (slab == slabs - 1), 0.0, 1.0)
    x_scale = jnp.where(is_odd, 0.0625, jnp.where(slab > 0, -0.0625, 0.0))
    yz_scale = jnp.where(is_odd, 0.0625, 0.0)
    for start in range(0, height, CHUNK):
        rows = slice(start, start + CHUNK)
        values = other_ref[left, rows]
        for label, half in enumerate(project_simplex(attraction(values, terms), 0.5)):
            known = h_ref[label, odd, rows]
            store_padded(n_ref, (label, 0), start, jnp.where(is_odd, known, half), height)
            n_ref[label, 1, rows] = jnp.where(is_odd, half, known)
    for label in range(labels):
        x, y, z = gradient(n_ref, label, 0, height, depth, open_z)
        x = x * open_x
        shrink = shrink_of(x, y, z)
        back = behind_yz(y * shrink, z * shrink, y_ref, (label,), height)
        n_ref[label, 1, 0:height] = x_scale * (x * shrink) + yz_scale * back
    sums = [sums_in[index] for index in range(2 * labels)]
    for start in range(0, height, CHUNK):
        rows = slice(start, start + CHUNK)
        values = v_ref[odd, rows]
        entries = [e_ref[label, rows] + n_ref[label, 1, rows] for label in range(labels)]
        for label, value in enumerate(project_simplex(entries, 0.5)):
            add_to(sums, label, value)
            add_to(sums, labels + label, value * values)
    lane = lax.broadcasted_iota(jnp.int32, (CHUNK, depth), 1)
    first = jnp.where(block > 0, 0, -1)
    last = jnp.where(block < blocks - 1, depth - 1, depth)
    keep = (lane != first) & (lane != last)
    sums = [jnp.where(keep, value, 0.0) for value in sums]
    out_ref[pl.ds(ROWS - 1, devices, stride=ROWS), :] = jnp.broadcast_to(
        pack_sums(sums, (1, lanes)), (devices, lanes)
    )


def ahead_kernel(
    v_ref, pair_ref, other_ref, base_ref, w_ref, q_ref, h_ref, s_ref, dual_ref, y_ref, l_ref
):
    slabs = lax.axis_size(SLABS)
    slab = slab_index()
    thick, height, depth = v_ref.shape
    lanes = thick * height
    labels = base_ref.shape[0]
    terms = affine(base_of(base_ref), 0.5)
    open_z = open_lanes(depth)
    halo = thick
    layers = thick + 2 * halo
    read = volume_layers(v_ref, pair_ref, other_ref, halo)

    first_halves(read, range(layers), height, terms, h_ref)
    inside = (slab > 0).astype(jnp.float32)
    open_x = (slab < slabs - 1).astype(jnp.float32)
    end = halo + thick - 1
    for label in range(labels):
        before = None
        for layer in range(layers - 1):
            x, y, z = gradient(h_ref, label, layer, height, depth, open_z)
            if layer == end:
                x = x * open_x
            shrink = shrink_of(x, y, z)
            x = x * shrink
            if layer == halo - 1:
                x = x * inside
            if layer:
                y, z = y * shrink, z * shrink
                where = (label, layer)
                dual_ref[label, 0, layer] = x
                dual_ref[label, 1, layer] = y
                dual_ref[label, 2, layer] = z
                l_ref[where] = (x - before) + behind_yz(y, z, y_ref, where, height)
            before = x
    for layer in range(1, layers - 1):
        for start in range(0, height, CHUNK):
            rows = slice(start, start + CHUNK)
            values = read(layer, rows)
            halves = [h_ref[label, layer, rows] for label in range(labels)]
            entries = [
                halves[label] + 0.0625 * l_ref[label, layer, rows] + term
                for label, term in enumerate(attraction(values, terms))
            ]
            for label, value in enumerate(project_simplex(entries, 0.5)):
                value = value + value
                store_padded(s_ref, (label, layer), start, value - halves[label], height)
                l_ref[label, layer, rows] = value
    for label in range(labels):
        before = None
        for layer in range(halo - 1, halo + thick):
            x, y, z = gradient(s_ref, label, layer, height, depth, open_z)
            if layer == end:
                x = x * open_x
            x = dual_ref[label, 0, layer] + x
            y = dual_ref[label, 1, layer] + y
            z = dual_ref[label, 2, layer] + z
            shrink = shrink_of(x, y, z)
            x = x * shrink
            if layer == halo - 1:
                x = x * inside
            else:
                divergence = (x - before) + behind_yz(
                    y * shrink, z * shrink, y_ref, (label, layer), height
                )
                w_ref[label, layer - halo] = l_ref[label, layer] + 0.125 * divergence
            before = x
    row = lax.broadcasted_iota(jnp.int32, (8, lanes), 0)
    near, far = [], []
    for start in (0, halo, halo + thick):
        turned = jnp.transpose(
            jnp.concatenate([read(start + index) for index in range(thick)], axis=0)
        )
        near.append(turned[0:8])
        far.append(turned[depth - 8 : depth])
    for column in range(6):
        plane = jnp.zeros((8, lanes), jnp.float32)
        for which in range(3):
            if column >= 2:
                plane = jnp.where(row == which, near[which][column - 2 : column - 1], plane)
            if column < 4:
                plane = jnp.where(row == 4 + which, far[which][4 + column : 5 + column], plane)
        q_ref[column] = plane


def last_kernel(v_ref, w_ref, q_ref, base_ref, got_ref, sums_ref, *rest):
    slabs = lax.axis_size(SLABS)
    blocks = lax.axis_size("gz")
    count = lax.axis_size("gy")
    groups = lax.axis_size("gx")
    slab, block = slab_index(), lax.axis_index("gz")
    pieces, lab_ref = rest[:count], rest[count]
    thick, height, depth = v_ref.shape
    lanes = thick * height
    labels = base_ref.shape[0]
    base = base_of(base_ref)
    terms = affine(base, 0.5)
    devices = slabs * blocks
    x_total = slabs * thick

    row = lax.broadcasted_iota(jnp.int32, (slabs, lanes), 0)
    everywhere = Planes((slabs, lanes), height, thick * row, x_total)
    sums = [None] * (2 * labels)
    for end in range(blocks - 1):
        planes = []
        for beyond, which in ((0, 2), (0, 3), (1, 0), (1, 1)):
            start = (end + beyond) * ROWS + which
            planes.append(
                jnp.concatenate(
                    [
                        got_ref[
                            pl.ds(start + outer * blocks * ROWS, count, stride=groups * blocks * ROWS)
                        ]
                        for outer in range(groups)
                    ],
                    axis=0,
                )
            )
        pulls = [attraction(plane, terms) for plane in planes]
        first = [project_simplex(pull, 0.5) for pull in pulls]
        divergence = [[], []]
        for label in range(labels):
            duals = [
                everywhere.dual(first[index][label], first[index + 1][label])
                for index in range(3)
            ]
            for index in (1, 2):
                x, y, z = duals[index]
                divergence[index - 1].append(
                    everywhere.behind_xy(x, y) + (z - duals[index - 1][2])
                )
        for index in (1, 2):
            entries = [
                first[index][label] + 0.0625 * divergence[index - 1][label] + pulls[index][label]
                for label in range(labels)
            ]
            for label, value in enumerate(project_simplex(entries, 0.5)):
                add_to(sums, label, value)
                add_to(sums, labels + label, value * planes[index])
    parts = got_ref[pl.ds(ROWS - 1, devices, stride=ROWS), :]
    lane = lax.broadcasted_iota(jnp.int32, (1, lanes), 1)
    parts = jnp.sum(parts, axis=0, keepdims=True)
    whole = []
    for index in range(2 * labels):
        part = jnp.where(lane == index, parts, 0.0)
        if blocks > 1:
            part = part + jnp.sum(sums[index], axis=0, keepdims=True)
        whole.append(2.0 * jnp.sum(part, axis=1, keepdims=True))
    centers = [
        (whole[labels + label] + prior_weight * base[label]) / (whole[label] + prior_weight)
        for label in range(labels)
    ]

    row = lax.broadcasted_iota(jnp.int32, (8, lanes), 0)
    local = Planes((8, lanes), height, thick * (slab - 1 + (row & 3)), x_total)
    planes = [q_ref[column] for column in range(6)]
    for which in range(3):
        index = rank_of(jnp.clip(slab - 1 + which, 0, slabs - 1)) * blocks
        low = (index + jnp.maximum(block - 1, 0)) * ROWS
        high = (index + jnp.minimum(block + 1, blocks - 1)) * ROWS
        for column in range(2):
            source = got_ref[pl.ds(low + 2 + column, 1), :]
            planes[column] = jnp.where(row == which, source, planes[column])
            source = got_ref[pl.ds(high + column, 1), :]
            planes[4 + column] = jnp.where(row == 4 + which, source, planes[4 + column])
    pulls = [attraction(plane, terms) for plane in planes]
    first = [project_simplex(pull, 0.5) for pull in pulls]
    duals = []
    for label in range(labels):
        duals.append([])
        for column in range(5):
            x, y, z = local.dual(first[column][label], first[column + 1][label])
            duals[label].append((x * local.inside, y, z))
    second, smooth = {}, {}
    for column in range(1, 5):
        entries = []
        for label in range(labels):
            x, y, z = duals[label][column]
            divergence = local.behind_xy(x, y) + (z - duals[label][column - 1][2])
            entries.append(first[column][label] + 0.0625 * divergence + pulls[column][label])
        second[column] = [value + value for value in project_simplex(entries, 0.5)]
        smooth[column] = [
            second[column][label] - first[column][label] for label in range(labels)
        ]
    for label in range(labels):
        for column in range(1, 4):
            x, y, z = local.dual(
                smooth[column][label], smooth[column + 1][label], duals[label][column]
            )
            duals[label][column] = (x * local.inside, y, z)
    terms = affine(centers, 1.0)
    edge = {}
    for column in (2, 3):
        pull = attraction(planes[column], terms)
        entries = []
        for label in range(labels):
            x, y, z = duals[label][column]
            divergence = local.behind_xy(x, y) + (z - duals[label][column - 1][2])
            entries.append(second[column][label] + 0.125 * divergence + pull[label])
        edge[column] = project_simplex(entries, 1.0)
    step = depth // labels
    tiles = [jnp.zeros((8, lanes), jnp.float32) for _ in range(depth // 8)]
    for label in range(labels):
        two, three = edge[2][label], edge[3][label]
        place = label * step // 8
        tiles[place] = tiles[place] + jnp.where(
            row == 0, pltpu.roll(two, 7, 0), jnp.where(row == 1, three, 0.0)
        )
        place = (place - 1) % (depth // 8)
        tiles[place] = tiles[place] + jnp.where(
            row == 6, pltpu.roll(two, 1, 0), jnp.where(row == 7, pltpu.roll(three, 2, 0), 0.0)
        )
    columns = jnp.transpose(jnp.concatenate(tiles, axis=0))

    z = lax.broadcasted_iota(jnp.int32, (CHUNK, depth), 1)
    replaced = ((z < 2) & (block > 0)) | ((z >= depth - 2) & (block < blocks - 1))
    sums = [None] * (2 * labels)
    for layer in range(thick):
        for start in range(0, height, CHUNK):
            rows = slice(start, start + CHUNK)
            values = v_ref[layer, rows]
            entries = [
                w_ref[label, layer, rows] + pull
                for label, pull in enumerate(attraction(values, terms))
            ]
            for label, value in enumerate(project_simplex(entries, 1.0)):
                column = columns[layer * height + start : layer * height + start + CHUNK]
                if label:
                    column = pltpu.roll(column, depth - label * step, 1)
                value = jnp.where(replaced, column, value)
                lab_ref[label, layer, rows] = value
                add_to(sums, label, value)
                add_to(sums, labels + label, value * values)
    sums_ref[...] = jnp.broadcast_to(pack_sums(sums, (1, lanes)), (devices, lanes))
    rows = height // count
    me = lax.axis_index("gy")
    for other in range(count):
        start = pl.multiple_of((me ^ other) * rows, rows)
        pieces[other][...] = lab_ref[:, :, pl.ds(start, rows), :]


def join_kernel(*refs):
    *pieces, out_ref = refs
    me = lax.axis_index("gy")
    thick = pieces[0].shape[1]
    for other, piece in enumerate(pieces):
        out_ref[:, pl.ds((me ^ other) * thick, thick)] = piece[...]


def local(volume, levels):
    slabs = lax.axis_size(SLABS)
    blocks = lax.axis_size("gz")
    count = lax.axis_size("gy")
    devices = slabs * blocks
    thick, height, depth = volume.shape
    labels = levels.shape[0]
    lanes = thick * height
    if thick != 2 or labels != 4 or count & (count - 1):
        raise ValueError("unsupported sizes")
    f32 = functools.partial(jax.ShapeDtypeStruct, dtype=jnp.float32)
    vmem = pl.BlockSpec(memory_space=pltpu.VMEM)

    base_levels = levels.astype(jnp.float32) / 255.0
    params = pltpu.CompilerParams(vmem_limit_bytes=8 << 20)
    base = pl.pallas_call(
        base_kernel,
        out_shape=f32((labels, lanes)),
        in_specs=[vmem],
        out_specs=vmem,
        compiler_params=params,
        cost_estimate=pl.CostEstimate(flops=COVER, bytes_accessed=0, transcendentals=0),
        name="base",
    )(levels.reshape(1, labels))

    pairs = [(i, i ^ 1) for i in range(slabs)]
    across = [(i, (i + 1) % slabs) for i in range(1, slabs, 2)]
    across += [(target, source) for source, target in across]
    pair = lax.ppermute(volume, SLABS, pairs)
    other = lax.ppermute(volume, SLABS, across)

    halves, entries, parts, edges = pl.pallas_call(
        pair_kernel,
        out_shape=[
            f32((labels, thick + 1, height + 8, depth)),
            f32((labels, height, depth)),
            f32((2 * labels, CHUNK, depth)),
            f32((4, lanes)),
        ],
        in_specs=[vmem] * 3,
        out_specs=[vmem] * 4,
        scratch_shapes=[
            pltpu.VMEM((labels, 2, height + 8, depth), jnp.float32),
            pltpu.VMEM((labels, 2, height, depth), jnp.float32),
            pltpu.VMEM((labels, 2, height, depth), jnp.float32),
        ],
        compiler_params=params,
        cost_estimate=pl.CostEstimate(flops=COVER, bytes_accessed=0, transcendentals=0),
        name="pair",
    )(volume, pair, base)
    sent = pl.pallas_call(
        first_kernel,
        out_shape=f32((devices * ROWS, lanes)),
        in_specs=[vmem] * 7,
        out_specs=vmem,
        scratch_shapes=[
            pltpu.VMEM((labels, 2, height + 8, depth), jnp.float32),
            pltpu.VMEM((labels, height + 8, depth), jnp.float32),
        ],
        compiler_params=params,
        name="first",
    )(volume, other, base, halves, entries, parts, edges)
    got = lax.all_to_all(sent.reshape(devices, 1, ROWS * lanes), AXES, 0, 0, tiled=True)
    got = got.reshape(devices * ROWS, lanes)

    layers = 3 * thick
    ahead, planes = pl.pallas_call(
        ahead_kernel,
        out_shape=[f32((labels, thick, height, depth)), f32((6, 8, lanes))],
        in_specs=[vmem] * 4,
        out_specs=[vmem] * 2,
        scratch_shapes=[
            pltpu.VMEM((labels, layers, height + 8, depth), jnp.float32),
            pltpu.VMEM((labels, layers, height + 8, depth), jnp.float32),
            pltpu.VMEM((labels, 3, layers, height, depth), jnp.float32),
            pltpu.VMEM((labels, layers, height + 8, depth), jnp.float32),
            pltpu.VMEM((labels, layers, height, depth), jnp.float32),
        ],
        cost_estimate=pl.CostEstimate(
            flops=200 * labels * layers * height * depth,
            bytes_accessed=4 * 20 * height * depth,
            transcendentals=0,
        ),
        compiler_params=params,
        name="ahead",
    )(volume, pair, other, base)

    piece = f32((labels, thick, height // count, depth))
    sums, *pieces = pl.pallas_call(
        last_kernel,
        out_shape=[f32((devices, lanes))] + [piece] * count,
        in_specs=[vmem] * 5,
        out_specs=[vmem] * (count + 1),
        scratch_shapes=[pltpu.VMEM((labels, thick, height, depth), jnp.float32)],
        compiler_params=params,
        name="last",
    )(volume, ahead, planes, base, got)

    total = lax.all_to_all(sums.reshape(devices, 1, lanes), AXES, 0, 0, tiled=True)
    for shift in range(1, count):
        pieces[shift] = lax.ppermute(pieces[shift], "gy", [(i, i ^ shift) for i in range(count)])
    join = pl.pallas_call(
        join_kernel,
        out_shape=f32((labels, thick * count, height // count, depth)),
        in_specs=[vmem] * count,
        out_specs=vmem,
        cost_estimate=pl.CostEstimate(
            flops=labels * thick * height * depth,
            bytes_accessed=8 * labels * thick * height * depth,
            transcendentals=0,
        ),
        compiler_params=params,
        name="join",
    )
    labelling = join(*pieces)
    total = total.sum((0, 1))
    sizes_all, weighted_all = total[:labels], total[labels : 2 * labels]
    centers = (weighted_all + prior_weight * base_levels) / (sizes_all + prior_weight)
    return (labelling, centers)


def solution(mesh):
    return jax.shard_map(
        local,
        mesh=mesh,
        in_specs=(P(("gx", "gy"), None, "gz"), P()),
        out_specs=(P(None, "gx", "gy", "gz"), P()),
        check_vma=False,
    )
```

profile of v0, /device:TPU:0, one launch (start us, length us, event | category | flops | bytes accessed | tf_op | source)
XLA Modules:
  0.0 33.8 jit_solution(17542981819188449221)
XLA Ops:
  0.6 0.0 copy-start.1
  0.6 0.6 %collective-permute-start = (f32[2,64,128]{2,1,0:T(8,128)}, f32[2,64,128]{2,1,0:T(8,128)S(1)}, u32[]{:S(2)}, u32[]{:S(2)}) collective-permute-start(f32[2,64,128]{2,1,0:T(8,128)} %v_ref.7), channel_id=1, source_target_pairs={{0,4},{4,0},{8,12},{12,8},{16,20},{20,16},{24,28},{28,24},{1,5},{5... | collective-permute-start | bytes 196616 | tf_op jit(solution)/shard_map/ppermute | solution.py:557
  1.2 3.5 %collective-permute-start.1 = (f32[2,64,128]{2,1,0:T(8,128)}, f32[2,64,128]{2,1,0:T(8,128)S(1)}, u32[]{:S(2)}, u32[]{:S(2)}) collective-permute-start(f32[2,64,128]{2,1,0:T(8,128)} %v_ref.7), channel_id=1, source_target_pairs={{4,8},{12,16},{20,24},{28,0},{8,4},{16,12},{24,20},{0,28},{5,9},{1... | collective-permute-start | bytes 196616 | tf_op jit(solution)/shard_map/ppermute | solution.py:558
  4.7 0.0 copy-done.1
  4.7 0.0 copy-start
  4.7 0.1 base.1.base_ref
  4.8 0.0 collective-permute-done.pair_ref
  4.8 0.8 %copy-done = f32[2,64,128]{2,1,0:T(8,128)S(1)} copy-done((f32[2,64,128]{2,1,0:T(8,128)S(1)}, f32[2,64,128]{2,1,0:T(8,128)}, u32[]{:S(2)}) %copy-start) | copy-done | bytes 65560
  5.6 0.6 %pair.1 = (f32[4,3,72,128]{3,2,1,0:T(8,128)S(1)}, f32[4,64,128]{2,1,0:T(8,128)S(1)}, f32[8,16,128]{2,1,0:T(8,128)S(1)}, f32[4,128]{1,0:T(4,128)S(1)}) custom-call(f32[2,64,128]{2,1,0:T(8,128)S(1)} %copy-done, f32[2,64,128]{2,1,0:T(8,128)S(1)} %collective-permute-done.pair_ref, f32[4,128]{1,0:T(4,128)S(1)} %base.1.base_ref), custom_call_target="tpu_custom_call" | custom-call | flops 50000000 | tf_op jit(solution)/shard_map/pair/pallas_call | solution.py:560
  6.2 0.7 %collective-permute-done.1.other_ref = f32[2,64,128]{2,1,0:T(8,128)S(1)} collective-permute-done((f32[2,64,128]{2,1,0:T(8,128)}, f32[2,64,128]{2,1,0:T(8,128)S(1)}, u32[]{:S(2)}, u32[]{:S(2)}) %collective-permute-start.1) | collective-permute-done | bytes 65568 | tf_op jit(solution)/shard_map/ppermute | solution.py:558
  7.0 1.0 %first.1 = f32[160,128]{1,0:T(8,128)} custom-call(f32[2,64,128]{2,1,0:T(8,128)S(1)} %copy-done, f32[2,64,128]{2,1,0:T(8,128)S(1)} %collective-permute-done.1.other_ref, f32[4,128]{1,0:T(4,128)S(1)} %base.1.base_ref, f32[4,3,72,128]{3,2,1,0:T(8,128)S(1)} %get-tuple-element.15.h_ref, f32[4,64,128]{2,1,0:T(8,128)S(1)} %get-tuple-element.16.e_ref, ...), custom_call_target="tpu_custom_call" | custom-call | tf_op jit(solution)/shard_map/first/pallas_call | solution.py:579
  7.9 6.0 %all-to-all-start = ((f32[32,1,640]{2,1,0:T(1,128)}), f32[32,1,640]{2,1,0:T(1,128)S(1)}, u32[]{:S(2)}, u32[]{:S(2)}) async-start(f32[32,1,640]{2,1,0:T(1,128)} %bitcast.1), calls=%async_computation | async-start | bytes 163840 | tf_op jit(solution)/shard_map/all_to_all | solution.py:591
  13.9 2.2 %ahead.1 = (f32[4,2,64,128]{3,2,1,0:T(8,128)S(1)}, f32[6,8,128]{2,1,0:T(8,128)S(1)}) custom-call(f32[2,64,128]{2,1,0:T(8,128)S(1)} %copy-done, f32[2,64,128]{2,1,0:T(8,128)S(1)} %collective-permute-done.pair_ref, f32[2,64,128]{2,1,0:T(8,128)S(1)} %collective-permute-done.1.other_ref, f32[4,128]{1,0:T(4,128)S(1)} %base.1.base_ref), custom_call_target="tpu_custom_call" | custom-call | flops 39321600 | bytes 655360 | tf_op jit(solution)/shard_map/ahead/pallas_call | solution.py:595
  16.1 5.2 %all-to-all-done = f32[32,1,640]{2,1,0:T(1,128)S(1)} async-done(((f32[32,1,640]{2,1,0:T(1,128)}), f32[32,1,640]{2,1,0:T(1,128)S(1)}, u32[]{:S(2)}, u32[]{:S(2)}) %all-to-all-start) | async-done | bytes 81952 | tf_op jit(solution)/shard_map/all_to_all | solution.py:591
  21.3 1.4 %last.1 = (f32[32,128]{1,0:T(8,128)}, f32[4,2,16,128]{3,2,1,0:T(8,128)S(1)}, f32[4,2,16,128]{3,2,1,0:T(8,128)S(1)}, f32[4,2,16,128]{3,2,1,0:T(8,128)S(1)}, f32[4,2,16,128]{3,2,1,0:T(8,128)S(1)}) custom-call(f32[2,64,128]{2,1,0:T(8,128)S(1)} %copy-done, f32[4,2,64,128]{3,2,1,0:T(8,128)S(1)} %get-tuple-element.13.w_ref, ...), custom_call_target="tpu_custom_call" | custom-call | tf_op jit(solution)/shard_map/last/pallas_call | solution.py:617
  22.8 2.5 %all-to-all-start.1 = ((f32[32,1,128]{2,1,0:T(1,128)}), f32[32,1,128]{2,1,0:T(1,128)S(1)}, u32[]{:S(2)}, u32[]{:S(2)}) async-start(f32[32,1,128]{2,1,0:T(1,128)} %bitcast.4), calls=%async_computation.1 | async-start | bytes 32768 | tf_op jit(solution)/shard_map/all_to_all | solution.py:627
  25.3 0.2 collective-permute-start.2
  25.5 1.6 %collective-permute-start.3 = (f32[4,2,16,128]{3,2,1,0:T(8,128)S(1)}, f32[4,2,16,128]{3,2,1,0:T(8,128)S(1)}, u32[]{:S(2)}, u32[]{:S(2)}) collective-permute-start(f32[4,2,16,128]{3,2,1,0:T(8,128)S(1)} %get-tuple-element.21), channel_id=1, source_target_pairs={{0,8},{4,12},{8,0},{12,4},{1,9},{5,13},{9,1},{13,5},{2,10},{6,14},... | collective-permute-start | bytes 196616 | tf_op jit(solution)/shard_map/ppermute | solution.py:629
  27.1 0.1 collective-permute-start.4
  27.2 5.1 %all-to-all-done.1 = f32[32,1,128]{2,1,0:T(1,128)S(1)} async-done(((f32[32,1,128]{2,1,0:T(1,128)}), f32[32,1,128]{2,1,0:T(1,128)S(1)}, u32[]{:S(2)}, u32[]{:S(2)}) %all-to-all-start.1) | async-done | bytes 16416 | tf_op jit(solution)/shard_map/all_to_all | solution.py:627
  32.4 0.1 reduce_sum.9
  32.4 0.6 %add_divide_fusion = f32[4]{0:T(128)} fusion(f32[128]{0:T(128)S(1)} %reduce_sum.9, s32[4]{0:T(128)S(1)} %copy-done.1), kind=kLoop, calls=%fused_computation | loop fusion | flops 20 | bytes 64 | tf_op jit(solution)/shard_map/div | solution.py:646
  33.0 0.0 collective-permute-done.2.refs_1_
  33.0 0.0 collective-permute-done.3.refs_2_
  33.0 0.0 collective-permute-done.4.refs_3_
  33.0 0.7 %join.1 = f32[4,8,16,128]{3,2,1,0:T(8,128)} custom-call(f32[4,2,16,128]{3,2,1,0:T(8,128)S(1)} %get-tuple-element.19.refs_0_, f32[4,2,16,128]{3,2,1,0:T(8,128)S(1)} %collective-permute-done.2.refs_1_, f32[4,2,16,128]{3,2,1,0:T(8,128)S(1)} %collective-permute-done.3.refs_2_, f32[4,2,16,128]{3,2,1,0:T(8,128)S(1)} %collective-permute-done.4.refs_3_), custom_call_target="tpu_custom_call" | custom-call | flops 65536 | bytes 524288 | tf_op jit(solution)/shard_map/join/pallas_call | solution.py:643
Async XLA Ops:
  0.6 4.1 %copy-start.1 = (s32[4]{0:T(128)S(1)}, s32[4]{0:T(128)}, u32[]{:S(2)}) copy-start(s32[4]{0:T(128)} %param.3) | copy-start | bytes 52
  0.6 4.2 %collective-permute-start = (f32[2,64,128]{2,1,0:T(8,128)}, f32[2,64,128]{2,1,0:T(8,128)S(1)}, u32[]{:S(2)}, u32[]{:S(2)}) collective-permute-start(f32[2,64,128]{2,1,0:T(8,128)} %v_ref.7), channel_id=1, source_target_pairs={{0,4},{4,0},{8,12},{12,8},{16,20},{20,16},{24,28},{28,24},{1,5},{5... | collective-permute-start | bytes 196616 | tf_op jit(solution)/shard_map/ppermute | solution.py:557
  1.2 5.8 %collective-permute-start.1 = (f32[2,64,128]{2,1,0:T(8,128)}, f32[2,64,128]{2,1,0:T(8,128)S(1)}, u32[]{:S(2)}, u32[]{:S(2)}) collective-permute-start(f32[2,64,128]{2,1,0:T(8,128)} %v_ref.7), channel_id=1, source_target_pairs={{4,8},{12,16},{20,24},{28,0},{8,4},{16,12},{24,20},{0,28},{5,9},{1... | collective-permute-start | bytes 196616 | tf_op jit(solution)/shard_map/ppermute | solution.py:558
  4.7 0.9 %copy-start = (f32[2,64,128]{2,1,0:T(8,128)S(1)}, f32[2,64,128]{2,1,0:T(8,128)}, u32[]{:S(2)}) copy-start(f32[2,64,128]{2,1,0:T(8,128)} %v_ref.7) | copy-start | bytes 196612
  7.9 13.4 %all-to-all-start = ((f32[32,1,640]{2,1,0:T(1,128)}), f32[32,1,640]{2,1,0:T(1,128)S(1)}, u32[]{:S(2)}, u32[]{:S(2)}) async-start(f32[32,1,640]{2,1,0:T(1,128)} %bitcast.1), calls=%async_computation | async-start | bytes 163840 | tf_op jit(solution)/shard_map/all_to_all | solution.py:591
  22.8 9.6 %all-to-all-start.1 = ((f32[32,1,128]{2,1,0:T(1,128)}), f32[32,1,128]{2,1,0:T(1,128)S(1)}, u32[]{:S(2)}, u32[]{:S(2)}) async-start(f32[32,1,128]{2,1,0:T(1,128)} %bitcast.4), calls=%async_computation.1 | async-start | bytes 32768 | tf_op jit(solution)/shard_map/all_to_all | solution.py:627
  25.3 7.7 %collective-permute-start.2 = (f32[4,2,16,128]{3,2,1,0:T(8,128)S(1)}, f32[4,2,16,128]{3,2,1,0:T(8,128)S(1)}, u32[]{:S(2)}, u32[]{:S(2)}) collective-permute-start(f32[4,2,16,128]{3,2,1,0:T(8,128)S(1)} %get-tuple-element.20), channel_id=1, source_target_pairs={{0,4},{4,0},{8,12},{12,8},{1,5},{5,1},{9,13},{13,9},{2,6},{6,2},{1... | collective-permute-start | bytes 196616 | tf_op jit(solution)/shard_map/ppermute | solution.py:629
  25.5 7.5 %collective-permute-start.3 = (f32[4,2,16,128]{3,2,1,0:T(8,128)S(1)}, f32[4,2,16,128]{3,2,1,0:T(8,128)S(1)}, u32[]{:S(2)}, u32[]{:S(2)}) collective-permute-start(f32[4,2,16,128]{3,2,1,0:T(8,128)S(1)} %get-tuple-element.21), channel_id=1, source_target_pairs={{0,8},{4,12},{8,0},{12,4},{1,9},{5,13},{9,1},{13,5},{2,10},{6,14},... | collective-permute-start | bytes 196616 | tf_op jit(solution)/shard_map/ppermute | solution.py:629
  27.1 5.9 %collective-permute-start.4 = (f32[4,2,16,128]{3,2,1,0:T(8,128)S(1)}, f32[4,2,16,128]{3,2,1,0:T(8,128)S(1)}, u32[]{:S(2)}, u32[]{:S(2)}) collective-permute-start(f32[4,2,16,128]{3,2,1,0:T(8,128)S(1)} %get-tuple-element.22), channel_id=1, source_target_pairs={{0,12},{4,8},{8,4},{12,0},{1,13},{5,9},{9,5},{13,1},{2,14},{6,10},... | collective-permute-start | bytes 196616 | tf_op jit(solution)/shard_map/ppermute | solution.py:629
where the time goes:
time: 34 us; the launch traced here: 33.8 us
  starting transfers between devices  14.6 us (43%)
  waiting for transfers between devices  11.1 us (33%)
  Pallas kernels  6.02 us (18%)
  local copies, waits for them, and re-layouts  0.8 us (2%)
  between operations  0.68 us (2%)
  other arithmetic  0.64 us (2%)
    all_to_all x1, starting transfers between devices, local(): lax.all_to_all(sent.reshape(devices, 1, ROWS * lanes), AXES, 0, 0, tiled=...  5.98 us
    all_to_all x1, waiting for transfers between devices, local(): lax.all_to_all(sent.reshape(devices, 1, ROWS * lanes), AXES, 0, 0, tiled=...  5.2 us
    all_to_all x1, waiting for transfers between devices, local(): lax.all_to_all(sums.reshape(devices, 1, lanes), AXES, 0, 0, tiled=True)  5.14 us
    ppermute x1, starting transfers between devices, local(): other = lax.ppermute(volume, SLABS, across)  3.54 us
    all_to_all x1, starting transfers between devices, local(): lax.all_to_all(sums.reshape(devices, 1, lanes), AXES, 0, 0, tiled=True)  2.54 us
    pallas_call x1, Pallas kernels, local(): pl.pallas_call(ahead_kernel, out_shape=[f32((labels, thick, height, depth...  2.21 us
    ppermute x3, starting transfers between devices, local(): lax.ppermute(pieces[shift], 'gy', [(i, i ^ shift) for i in range(count)])  1.93 us
    pallas_call x1, Pallas kernels, local(): pl.pallas_call(last_kernel, out_shape=[f32((devices, lanes))] + [piece] *...  1.42 us
  transfers between devices with their start and end apart: 7, of which 3 were waited for; matrix products, arithmetic and copies ran while one was open for 2% of the time, Pallas kernels for 9%

commit v1 on v0

--- a/solution.py
+++ b/solution.py
@@ -368,7 +368,7 @@
     count = lax.axis_size("gy")
     groups = lax.axis_size("gx")
     slab, block = slab_index(), lax.axis_index("gz")
-    pieces, lab_ref = rest[:count], rest[count]
+    pieces, (lab_ref, row_ref, left) = rest[:count], rest[count:]
     thick, height, depth = v_ref.shape
     lanes = thick * height
     labels = base_ref.shape[0]
@@ -510,12 +510,15 @@
                 lab_ref[label, layer, rows] = value
                 add_to(sums, label, value)
                 add_to(sums, labels + label, value * values)
-    sums_ref[...] = jnp.broadcast_to(pack_sums(sums, (1, lanes)), (devices, lanes))
+    row_ref[...] = jnp.broadcast_to(pack_sums(sums, (1, lanes)), (devices, lanes))
+    copy = pltpu.make_async_copy(row_ref, sums_ref, left)
+    copy.start()
     rows = height // count
     me = lax.axis_index("gy")
     for other in range(count):
         start = pl.multiple_of((me ^ other) * rows, rows)
         pieces[other][...] = lab_ref[:, :, pl.ds(start, rows), :]
+    copy.wait()
 
 
 def join_kernel(*refs):
@@ -618,8 +621,12 @@
         last_kernel,
         out_shape=[f32((devices, lanes))] + [piece] * count,
         in_specs=[vmem] * 5,
-        out_specs=[vmem] * (count + 1),
-        scratch_shapes=[pltpu.VMEM((labels, thick, height, depth), jnp.float32)],
+        out_specs=[pl.BlockSpec(memory_space=pltpu.HBM)] + [vmem] * count,
+        scratch_shapes=[
+            pltpu.VMEM((labels, thick, height, depth), jnp.float32),
+            pltpu.VMEM((devices, lanes), jnp.float32),
+            pltpu.SemaphoreType.DMA,
+        ],
         compiler_params=params,
         name="last",
     )(volume, ahead, planes, base, got)

time: 34 us -> 34 us (level)
  no operation moved by 1% of the time
where the time goes in v1:
time: 34 us; the launch traced here: 33.8 us
  starting transfers between devices  14.6 us (43%)
  waiting for transfers between devices  11.1 us (33%)
  Pallas kernels  6.03 us (18%)
  local copies, waits for them, and re-layouts  0.8 us (2%)
  between operations  0.69 us (2%)
  other arithmetic  0.64 us (2%)
    all_to_all x1, starting transfers between devices, local(): lax.all_to_all(sent.reshape(devices, 1, ROWS * lanes), AXES, 0, 0, tiled=...  5.98 us
    all_to_all x1, waiting for transfers between devices, local(): lax.all_to_all(sent.reshape(devices, 1, ROWS * lanes), AXES, 0, 0, tiled=...  5.2 us
    all_to_all x1, waiting for transfers between devices, local(): lax.all_to_all(sums.reshape(devices, 1, lanes), AXES, 0, 0, tiled=True)  5.14 us
    ppermute x1, starting transfers between devices, local(): other = lax.ppermute(volume, SLABS, across)  3.54 us
    all_to_all x1, starting transfers between devices, local(): lax.all_to_all(sums.reshape(devices, 1, lanes), AXES, 0, 0, tiled=True)  2.56 us
    pallas_call x1, Pallas kernels, local(): pl.pallas_call(ahead_kernel, out_shape=[f32((labels, thick, height, depth...  2.21 us
    ppermute x3, starting transfers between devices, local(): lax.ppermute(pieces[shift], 'gy', [(i, i ^ shift) for i in range(count)])  1.93 us
    pallas_call x1, Pallas kernels, local(): pl.pallas_call(last_kernel, out_shape=[f32((devices, lanes))] + [piece] *...  1.43 us
  transfers between devices with their start and end apart: 7, of which 3 were waited for; matrix products, arithmetic and copies ran while one was open for 2% of the time, Pallas kernels for 9%

profile of v1, /device:TPU:0, one launch (start us, length us, event | category | flops | bytes accessed | tf_op | source)
XLA Modules:
  0.0 33.8 jit_solution(6209006726969333494)
XLA Ops:
  0.6 0.0 copy-start.1
  0.6 0.6 %collective-permute-start = (f32[2,64,128]{2,1,0:T(8,128)}, f32[2,64,128]{2,1,0:T(8,128)S(1)}, u32[]{:S(2)}, u32[]{:S(2)}) collective-permute-start(f32[2,64,128]{2,1,0:T(8,128)} %v_ref.7), channel_id=1, source_target_pairs={{0,4},{4,0},{8,12},{12,8},{16,20},{20,16},{24,28},{28,24},{1,5},{5... | collective-permute-start | bytes 196616 | tf_op jit(solution)/shard_map/ppermute | solution.py:560
  1.2 3.5 %collective-permute-start.1 = (f32[2,64,128]{2,1,0:T(8,128)}, f32[2,64,128]{2,1,0:T(8,128)S(1)}, u32[]{:S(2)}, u32[]{:S(2)}) collective-permute-start(f32[2,64,128]{2,1,0:T(8,128)} %v_ref.7), channel_id=1, source_target_pairs={{4,8},{12,16},{20,24},{28,0},{8,4},{16,12},{24,20},{0,28},{5,9},{1... | collective-permute-start | bytes 196616 | tf_op jit(solution)/shard_map/ppermute | solution.py:561
  4.7 0.0 copy-done.1
  4.7 0.0 copy-start
  4.7 0.1 base.1.base_ref
  4.8 0.0 collective-permute-done.pair_ref
  4.8 0.8 %copy-done = f32[2,64,128]{2,1,0:T(8,128)S(1)} copy-done((f32[2,64,128]{2,1,0:T(8,128)S(1)}, f32[2,64,128]{2,1,0:T(8,128)}, u32[]{:S(2)}) %copy-start) | copy-done | bytes 65560
  5.6 0.6 %pair.1 = (f32[4,3,72,128]{3,2,1,0:T(8,128)S(1)}, f32[4,64,128]{2,1,0:T(8,128)S(1)}, f32[8,16,128]{2,1,0:T(8,128)S(1)}, f32[4,128]{1,0:T(4,128)S(1)}) custom-call(f32[2,64,128]{2,1,0:T(8,128)S(1)} %copy-done, f32[2,64,128]{2,1,0:T(8,128)S(1)} %collective-permute-done.pair_ref, f32[4,128]{1,0:T(4,128)S(1)} %base.1.base_ref), custom_call_target="tpu_custom_call" | custom-call | flops 50000000 | tf_op jit(solution)/shard_map/pair/pallas_call | solution.py:563
  6.2 0.7 %collective-permute-done.1.other_ref = f32[2,64,128]{2,1,0:T(8,128)S(1)} collective-permute-done((f32[2,64,128]{2,1,0:T(8,128)}, f32[2,64,128]{2,1,0:T(8,128)S(1)}, u32[]{:S(2)}, u32[]{:S(2)}) %collective-permute-start.1) | collective-permute-done | bytes 65568 | tf_op jit(solution)/shard_map/ppermute | solution.py:561
  7.0 1.0 %first.1 = f32[160,128]{1,0:T(8,128)} custom-call(f32[2,64,128]{2,1,0:T(8,128)S(1)} %copy-done, f32[2,64,128]{2,1,0:T(8,128)S(1)} %collective-permute-done.1.other_ref, f32[4,128]{1,0:T(4,128)S(1)} %base.1.base_ref, f32[4,3,72,128]{3,2,1,0:T(8,128)S(1)} %get-tuple-element.15.h_ref, f32[4,64,128]{2,1,0:T(8,128)S(1)} %get-tuple-element.16.e_ref, ...), custom_call_target="tpu_custom_call" | custom-call | tf_op jit(solution)/shard_map/first/pallas_call | solution.py:582
  7.9 6.0 %all-to-all-start = ((f32[32,1,640]{2,1,0:T(1,128)}), f32[32,1,640]{2,1,0:T(1,128)S(1)}, u32[]{:S(2)}, u32[]{:S(2)}) async-start(f32[32,1,640]{2,1,0:T(1,128)} %bitcast.1), calls=%async_computation | async-start | bytes 163840 | tf_op jit(solution)/shard_map/all_to_all | solution.py:594
  13.9 2.2 %ahead.1 = (f32[4,2,64,128]{3,2,1,0:T(8,128)S(1)}, f32[6,8,128]{2,1,0:T(8,128)S(1)}) custom-call(f32[2,64,128]{2,1,0:T(8,128)S(1)} %copy-done, f32[2,64,128]{2,1,0:T(8,128)S(1)} %collective-permute-done.pair_ref, f32[2,64,128]{2,1,0:T(8,128)S(1)} %collective-permute-done.1.other_ref, f32[4,128]{1,0:T(4,128)S(1)} %base.1.base_ref), custom_call_target="tpu_custom_call" | custom-call | flops 39321600 | bytes 655360 | tf_op jit(solution)/shard_map/ahead/pallas_call | solution.py:598
  16.1 5.2 %all-to-all-done = f32[32,1,640]{2,1,0:T(1,128)S(1)} async-done(((f32[32,1,640]{2,1,0:T(1,128)}), f32[32,1,640]{2,1,0:T(1,128)S(1)}, u32[]{:S(2)}, u32[]{:S(2)}) %all-to-all-start) | async-done | bytes 81952 | tf_op jit(solution)/shard_map/all_to_all | solution.py:594
  21.3 1.4 %last.1 = (f32[32,128]{1,0:T(8,128)}, f32[4,2,16,128]{3,2,1,0:T(8,128)S(1)}, f32[4,2,16,128]{3,2,1,0:T(8,128)S(1)}, f32[4,2,16,128]{3,2,1,0:T(8,128)S(1)}, f32[4,2,16,128]{3,2,1,0:T(8,128)S(1)}) custom-call(f32[2,64,128]{2,1,0:T(8,128)S(1)} %copy-done, f32[4,2,64,128]{3,2,1,0:T(8,128)S(1)} %get-tuple-element.13.w_ref, ...), custom_call_target="tpu_custom_call" | custom-call | tf_op jit(solution)/shard_map/last/pallas_call | solution.py:620
  22.8 2.6 %all-to-all-start.1 = ((f32[32,1,128]{2,1,0:T(1,128)}), f32[32,1,128]{2,1,0:T(1,128)S(1)}, u32[]{:S(2)}, u32[]{:S(2)}) async-start(f32[32,1,128]{2,1,0:T(1,128)} %bitcast.4), calls=%async_computation.1 | async-start | bytes 32768 | tf_op jit(solution)/shard_map/all_to_all | solution.py:634
  25.4 0.2 collective-permute-start.2
  25.5 1.6 %collective-permute-start.3 = (f32[4,2,16,128]{3,2,1,0:T(8,128)S(1)}, f32[4,2,16,128]{3,2,1,0:T(8,128)S(1)}, u32[]{:S(2)}, u32[]{:S(2)}) collective-permute-start(f32[4,2,16,128]{3,2,1,0:T(8,128)S(1)} %get-tuple-element.21), channel_id=1, source_target_pairs={{0,8},{4,12},{8,0},{12,4},{1,9},{5,13},{9,1},{13,5},{2,10},{6,14},... | collective-permute-start | bytes 196616 | tf_op jit(solution)/shard_map/ppermute | solution.py:636
  27.2 0.1 collective-permute-start.4
  27.3 5.1 %all-to-all-done.1 = f32[32,1,128]{2,1,0:T(1,128)S(1)} async-done(((f32[32,1,128]{2,1,0:T(1,128)}), f32[32,1,128]{2,1,0:T(1,128)S(1)}, u32[]{:S(2)}, u32[]{:S(2)}) %all-to-all-start.1) | async-done | bytes 16416 | tf_op jit(solution)/shard_map/all_to_all | solution.py:634
  32.4 0.1 reduce_sum.9
  32.5 0.6 %add_divide_fusion = f32[4]{0:T(128)} fusion(f32[128]{0:T(128)S(1)} %reduce_sum.9, s32[4]{0:T(128)S(1)} %copy-done.1), kind=kLoop, calls=%fused_computation | loop fusion | flops 20 | bytes 64 | tf_op jit(solution)/shard_map/div | solution.py:653
  33.1 0.0 collective-permute-done.2.refs_1_
  33.1 0.0 collective-permute-done.3.refs_2_
  33.1 0.0 collective-permute-done.4.refs_3_
  33.1 0.7 %join.1 = f32[4,8,16,128]{3,2,1,0:T(8,128)} custom-call(f32[4,2,16,128]{3,2,1,0:T(8,128)S(1)} %get-tuple-element.19.refs_0_, f32[4,2,16,128]{3,2,1,0:T(8,128)S(1)} %collective-permute-done.2.refs_1_, f32[4,2,16,128]{3,2,1,0:T(8,128)S(1)} %collective-permute-done.3.refs_2_, f32[4,2,16,128]{3,2,1,0:T(8,128)S(1)} %collective-permute-done.4.refs_3_), custom_call_target="tpu_custom_call" | custom-call | flops 65536 | bytes 524288 | tf_op jit(solution)/shard_map/join/pallas_call | solution.py:650
Async XLA Ops:
  0.6 4.1 %copy-start.1 = (s32[4]{0:T(128)S(1)}, s32[4]{0:T(128)}, u32[]{:S(2)}) copy-start(s32[4]{0:T(128)} %param.3) | copy-start | bytes 52
  0.6 4.2 %collective-permute-start = (f32[2,64,128]{2,1,0:T(8,128)}, f32[2,64,128]{2,1,0:T(8,128)S(1)}, u32[]{:S(2)}, u32[]{:S(2)}) collective-permute-start(f32[2,64,128]{2,1,0:T(8,128)} %v_ref.7), channel_id=1, source_target_pairs={{0,4},{4,0},{8,12},{12,8},{16,20},{20,16},{24,28},{28,24},{1,5},{5... | collective-permute-start | bytes 196616 | tf_op jit(solution)/shard_map/ppermute | solution.py:560
  1.2 5.8 %collective-permute-start.1 = (f32[2,64,128]{2,1,0:T(8,128)}, f32[2,64,128]{2,1,0:T(8,128)S(1)}, u32[]{:S(2)}, u32[]{:S(2)}) collective-permute-start(f32[2,64,128]{2,1,0:T(8,128)} %v_ref.7), channel_id=1, source_target_pairs={{4,8},{12,16},{20,24},{28,0},{8,4},{16,12},{24,20},{0,28},{5,9},{1... | collective-permute-start | bytes 196616 | tf_op jit(solution)/shard_map/ppermute | solution.py:561
  4.7 0.9 %copy-start = (f32[2,64,128]{2,1,0:T(8,128)S(1)}, f32[2,64,128]{2,1,0:T(8,128)}, u32[]{:S(2)}) copy-start(f32[2,64,128]{2,1,0:T(8,128)} %v_ref.7) | copy-start | bytes 196612
  7.9 13.4 %all-to-all-start = ((f32[32,1,640]{2,1,0:T(1,128)}), f32[32,1,640]{2,1,0:T(1,128)S(1)}, u32[]{:S(2)}, u32[]{:S(2)}) async-start(f32[32,1,640]{2,1,0:T(1,128)} %bitcast.1), calls=%async_computation | async-start | bytes 163840 | tf_op jit(solution)/shard_map/all_to_all | solution.py:594
  22.8 9.6 %all-to-all-start.1 = ((f32[32,1,128]{2,1,0:T(1,128)}), f32[32,1,128]{2,1,0:T(1,128)S(1)}, u32[]{:S(2)}, u32[]{:S(2)}) async-start(f32[32,1,128]{2,1,0:T(1,128)} %bitcast.4), calls=%async_computation.1 | async-start | bytes 32768 | tf_op jit(solution)/shard_map/all_to_all | solution.py:634
  25.4 7.7 %collective-permute-start.2 = (f32[4,2,16,128]{3,2,1,0:T(8,128)S(1)}, f32[4,2,16,128]{3,2,1,0:T(8,128)S(1)}, u32[]{:S(2)}, u32[]{:S(2)}) collective-permute-start(f32[4,2,16,128]{3,2,1,0:T(8,128)S(1)} %get-tuple-element.20), channel_id=1, source_target_pairs={{0,4},{4,0},{8,12},{12,8},{1,5},{5,1},{9,13},{13,9},{2,6},{6,2},{1... | collective-permute-start | bytes 196616 | tf_op jit(solution)/shard_map/ppermute | solution.py:636
  25.5 7.5 %collective-permute-start.3 = (f32[4,2,16,128]{3,2,1,0:T(8,128)S(1)}, f32[4,2,16,128]{3,2,1,0:T(8,128)S(1)}, u32[]{:S(2)}, u32[]{:S(2)}) collective-permute-start(f32[4,2,16,128]{3,2,1,0:T(8,128)S(1)} %get-tuple-element.21), channel_id=1, source_target_pairs={{0,8},{4,12},{8,0},{12,4},{1,9},{5,13},{9,1},{13,5},{2,10},{6,14},... | collective-permute-start | bytes 196616 | tf_op jit(solution)/shard_map/ppermute | solution.py:636
  27.2 5.9 %collective-permute-start.4 = (f32[4,2,16,128]{3,2,1,0:T(8,128)S(1)}, f32[4,2,16,128]{3,2,1,0:T(8,128)S(1)}, u32[]{:S(2)}, u32[]{:S(2)}) collective-permute-start(f32[4,2,16,128]{3,2,1,0:T(8,128)S(1)} %get-tuple-element.22), channel_id=1, source_target_pairs={{0,12},{4,8},{8,4},{12,0},{1,13},{5,9},{9,5},{13,1},{2,14},{6,10},... | collective-permute-start | bytes 196616 | tf_op jit(solution)/shard_map/ppermute | solution.py:636
